TPU v7x, 32 devices: a whole 2x2x4 slice. The times are simulated.
32 devices in a mesh: member: 2 (over core), section: 4 (over y, x), atoms: 4 (over z).
Axes of the slice: x: 2, y: 2, z: 4, core: 2. Of those that a mesh axis runs over, the one named last changes fastest.
Arguments:
- positions: float32 [8, 3, 512], P(None, None, 'atoms'), may hold values from -8 to 8
- atom_types: int32 [8, 512], P(None, 'atoms'), may hold values from 0 to 127
- neighbors: int32 [8, 512, 128], P(None, 'atoms'), may hold values from 0 to 511
- nbr_mask: int32 [8, 512, 128], P(None, 'atoms'), may hold values 0 or 1
- type_table: bfloat16 [2, 128, 128], P('member'), may hold values from -6 to 6
- norm_gain: bfloat16 [2, 4, 128], P('member', 'section'), may hold values from 0.25 to 1.75
- proj_weight: bfloat16 [2, 4, 128, 384], P('member', 'section'), may hold values from -0.5 to 0.5
- out_weight: bfloat16 [2, 4, 128, 128], P('member', 'section'), may hold values from -0.5 to 0.5
- force_coef: bfloat16 [2, 4, 4], P('member', 'section'), may hold values from -48 to 48
Outputs:
- atom_dev: float32 [8, 512], P('section', 'atoms')
- max_dev: float32 [8], P('section')
- mean_force: float32 [8, 3, 512], P('section', None, 'atoms')
Inputs may be any that keep to these rules, and one draw needn't show every extreme that they name: `neighbors`: indices of atoms of the same frame, repeats and the atom itself allowed.
All inputs are finite; a program needn't handle non-finite values. No bound on the sum of `nbr_mask` on one device may be relied on, other than what follows from the above.
Results may differ from a plain program's by a relative error of at most 0.013.
Values may be sent and summed in bfloat16 or wider, within the bound.
No kernel may reach another device: no remote copies, remote signals or barrier semaphores. Data moves between devices by JAX's collectives and lax.ppermute only.
A program may use at most 64 MiB of HBM per device.

v0:
```python
import math
import jax
import jax.numpy as jnp
from jax import lax
from jax.sharding import PartitionSpec as P


def geometry(nbr, mask, pos_all, pos_own):
    total_atoms = pos_all.shape[1]
    hit = (nbr[:, :, None] == lax.iota(jnp.int32, total_atoms)[None, None, :]).astype(jnp.float32)
    counts = jnp.sum(hit * mask.astype(jnp.float32)[:, :, None], 1)
    delta = pos_all[:, None, :] - pos_own[:, :, None]
    switch = 1.0 / (1.0 + 0.125 * jnp.sum(delta * delta, 0))
    return (counts * switch, delta)


def block_dev(h_in, gain, proj, outw, coef, pair, delta, slots):
    width = h_in.shape[1]
    heads = coef.shape[0]
    head_dim = width // heads
    count = h_in.shape[0]
    hf = h_in.astype(jnp.float32)
    normed = (
        hf * lax.rsqrt(jnp.mean(hf * hf, -1, keepdims=True) + 1e-06) * gain.astype(jnp.float32)
    ).astype(jnp.bfloat16)
    query = jnp.dot(normed, proj[:, :width], preferred_element_type=jnp.float32).astype(
        jnp.bfloat16
    )
    keyval = jnp.dot(
        lax.all_gather(normed, "atoms", axis=0, tiled=True),
        proj[:, width:],
        preferred_element_type=jnp.float32,
    ).astype(jnp.bfloat16)
    total_atoms = keyval.shape[0]
    query3 = query.reshape(count, heads, head_dim)
    keys = keyval[:, :width].reshape(total_atoms, heads, head_dim)
    values = keyval[:, width:].reshape(total_atoms, heads, head_dim)
    scores = jnp.einsum(
        "ahd,jhd->haj", query3, keys, preferred_element_type=jnp.float32
    ) / math.sqrt(head_dim)
    weights = jax.nn.sigmoid(scores) * pair[None]
    message = jnp.einsum(
        "haj,jhd->ahd", weights.astype(jnp.bfloat16), values, preferred_element_type=jnp.float32
    )
    message = (message / slots).reshape(count, width).astype(jnp.bfloat16)
    h_out = (hf + jnp.dot(message, outw, preferred_element_type=jnp.float32)).astype(jnp.bfloat16)
    pair_coef = jnp.einsum("h,haj->aj", coef.astype(jnp.float32), weights)
    force = jnp.einsum("aj,caj->ca", pair_coef, delta) / slots
    return (h_out, force)


def embed(types_now, table):
    onehot = (types_now[:, None] == lax.iota(jnp.int32, table.shape[0])[None, :]).astype(
        jnp.bfloat16
    )
    return jnp.dot(onehot, table, preferred_element_type=jnp.float32).astype(jnp.bfloat16)


def shards(
    positions,
    atom_types,
    neighbors,
    nbr_mask,
    type_table,
    norm_gain,
    proj_weight,
    out_weight,
    force_coef,
):
    n_section = lax.axis_size("section")
    section_idx = lax.axis_index("section")
    frames = atom_types.shape[0]
    per_section = frames // n_section
    count = atom_types.shape[1]
    slots = neighbors.shape[2]
    table = type_table[0]
    pos_all = lax.all_gather(positions, "atoms", axis=2, tiled=True)
    gains, projs, outs, coefs = (
        lax.all_gather(norm_gain, "section", axis=1, tiled=True),
        lax.all_gather(proj_weight, "section", axis=1, tiled=True),
        lax.all_gather(out_weight, "section", axis=1, tiled=True),
        lax.all_gather(force_coef, "section", axis=1, tiled=True),
    )
    first = section_idx * per_section

    def whole_frame(local, own_forces):
        frame = first + local
        nbr = lax.dynamic_index_in_dim(neighbors, frame, 0, keepdims=False)
        mask = lax.dynamic_index_in_dim(nbr_mask, frame, 0, keepdims=False)
        pos_now = lax.dynamic_index_in_dim(pos_all, frame, 0, keepdims=False)
        pos_own = lax.dynamic_index_in_dim(positions, frame, 0, keepdims=False)
        pair, delta = geometry(nbr, mask, pos_now, pos_own)
        h_cur = embed(lax.dynamic_index_in_dim(atom_types, frame, 0, keepdims=False), table)
        total = jnp.zeros((3, count), jnp.float32)
        for blk in range(n_section):
            h_cur, term = block_dev(
                h_cur, gains[0, blk], projs[0, blk], outs[0, blk], coefs[0, blk], pair, delta, slots
            )
            total = total + term
        return lax.dynamic_update_index_in_dim(own_forces, total, local, 0)

    own = lax.fori_loop(
        0, per_section, whole_frame, jnp.zeros((per_section, 3, count), jnp.float32)
    )
    members = lax.axis_size("member")
    mean_force = lax.psum(own, "member") / members
    centered = own - mean_force
    spread = lax.psum(jnp.sum(centered * centered, 1), "member") / members
    atom_dev = jnp.sqrt(spread)
    max_dev = lax.pmax(jnp.max(atom_dev, -1), "atoms")
    return (atom_dev, max_dev, mean_force)


def solution(mesh):
    return jax.shard_map(
        shards,
        mesh=mesh,
        in_specs=(
            P(None, None, "atoms"),
            P(None, "atoms"),
            P(None, "atoms", None),
            P(None, "atoms", None),
            P("member", None, None),
            P("member", "section", None),
            P("member", "section", None, None),
            P("member", "section", None, None),
            P("member", "section", None),
        ),
        out_specs=(P("section", "atoms"), P("section"), P("section", None, "atoms")),
        check_vma=False,
    )
```

profile of v0, /device:TPU:0, one launch (start us, length us, event | category | flops | bytes accessed | tf_op | source)
XLA Modules:
  0.0 200.3 jit_solution(8612434693529792498)
XLA Ops:
  0.6 9.5 %all_gather.44 = bf16[1,4,128]{2,0,1:T(2,128)(2,1)S(1)} all-gather(bf16[1,1,128]{2,0,1:T(2,128)(2,1)} %bitcast.301), channel_id=1, replica_groups=mesh['member'=2,'section'=4,'atoms'=4] {'section'}, dimensions={1}, use_global_device_ids=true | all-gather | bytes 1280 | tf_op jit(solution)/shard_map/all_gather | solution.py:79
  10.2 7.8 %all_gather.46 = bf16[1,4,4]{2,0,1:T(2,128)(2,1)S(1)} all-gather(bf16[1,1,4]{2,0,1:T(2,128)(2,1)} %bitcast.302), channel_id=1, replica_groups=mesh['member'=2,'section'=4,'atoms'=4] {'section'}, dimensions={1}, use_global_device_ids=true | all-gather | bytes 40 | tf_op jit(solution)/shard_map/all_gather | solution.py:82
  18.0 0.7 copy.31
  18.7 12.2 %all_gather.43 = f32[8,3,512]{2,1,0:T(4,128)S(1)} all-gather(f32[8,3,128]{2,1,0:T(4,128)S(1)} %copy.31), channel_id=1, replica_groups=mesh['member'=2,'section'=4,'atoms'=4] {'atoms'}, dimensions={2}, use_global_device_ids=true | all-gather | bytes 61440 | tf_op jit(solution)/shard_map/all_gather | solution.py:77
  30.9 7.7 %all_gather.47 = bf16[1,4,128,128]{3,2,0,1:T(8,128)(2,1)S(1)} all-gather(bf16[1,1,128,128]{3,2,0,1:T(8,128)(2,1)} %bitcast.300), channel_id=1, replica_groups=mesh['member'=2,'section'=4,'atoms'=4] {'section'}, dimensions={1}, use_global_device_ids=true | all-gather | bytes 163840 | tf_op jit(solution)/shard_map/all_gather | solution.py:81
  38.6 9.3 %all_gather.45 = bf16[1,4,128,384]{3,2,0,1:T(8,128)(2,1)S(1)} all-gather(bf16[1,1,128,384]{3,2,0,1:T(8,128)(2,1)} %bitcast.299), channel_id=1, replica_groups=mesh['member'=2,'section'=4,'atoms'=4] {'section'}, dimensions={1}, use_global_device_ids=true | all-gather | bytes 491520 | tf_op jit(solution)/shard_map/all_gather | solution.py:80
  47.9 137.4 %while.13 = (s32[]{:T(128)}, f32[2,3,128]{2,0,1:T(2,128)S(1)}, s32[]{:T(128)}, f32[8,3,512]{2,1,0:T(4,128)S(1)}, f32[8,3,128]{2,1,0:T(4,128)S(1)}, /*index=5*/s3...) while((s32[]{:T(128)}, f32[2,3,128]{2,0,1:T(2,128)S(1)}, ...), condition=%wide.region_7.8_spmd, body=%wide.region_0.7_spmd.sunk | while | flops 322554368 | bytes 20396256 | solution.py:102
  47.9 0.7 fusion.231
  49.0 0.9 convert_bitcast_fusion.2
  49.9 6.0 %select_reduce_fusion.2 = f32[128,512]{1,0:T(8,128)S(1)} fusion(f32[128,128]{1,0:T(8,128)S(1)} %get-tuple-element.420, s32[128,128]{1,0:T(8,128)S(1)} %get-tuple-element.421), kind=kLoop, calls=%fused_computation.clone.1 | loop fusion | flops 25100288 | bytes 393216 | tf_op jit(solution)/shard_map/while/body/eval_jaxpr/reduce_sum | solution.py:11
  55.8 12.3 %all_gather.52 = bf16[512,128]{0,1:T(8,128)(2,1)S(1)} all-gather(bf16[128,128]{0,1:T(8,128)(2,1)S(1)} %multiply_convert_fusion.8), channel_id=1, replica_groups=mesh['member'=2,'section'=4,'atoms'=4] {'atoms'}, dimensions={0}, use_global_device_ids=true | all-gather | bytes 163840 | tf_op jit(solution)/shard_map/while/body/eval_jaxpr/all_gather | solution.py:30
  71.6 12.3 %all_gather.53 = bf16[512,128]{0,1:T(8,128)(2,1)S(1)} all-gather(bf16[128,128]{0,1:T(8,128)(2,1)S(1)} %multiply_convert_fusion.9), channel_id=1, replica_groups=mesh['member'=2,'section'=4,'atoms'=4] {'atoms'}, dimensions={0}, use_global_device_ids=true | all-gather | bytes 163840 | tf_op jit(solution)/shard_map/while/body/eval_jaxpr/all_gather | solution.py:30
  86.8 12.3 %all_gather.54 = bf16[512,128]{0,1:T(8,128)(2,1)S(1)} all-gather(bf16[128,128]{0,1:T(8,128)(2,1)S(1)} %multiply_convert_fusion.10), channel_id=1, replica_groups=mesh['member'=2,'section'=4,'atoms'=4] {'atoms'}, dimensions={0}, use_global_device_ids=true | all-gather | bytes 163840 | tf_op jit(solution)/shard_map/while/body/eval_jaxpr/all_gather | solution.py:30
  101.9 12.5 %all_gather.55 = bf16[512,128]{0,1:T(8,128)(2,1)S(1)} all-gather(bf16[128,128]{0,1:T(8,128)(2,1)S(1)} %multiply_convert_fusion.11), channel_id=1, replica_groups=mesh['member'=2,'section'=4,'atoms'=4] {'atoms'}, dimensions={0}, use_global_device_ids=true | all-gather | bytes 163840 | tf_op jit(solution)/shard_map/while/body/eval_jaxpr/all_gather | solution.py:30
  116.5 0.7 fusion.231
  117.6 0.9 convert_bitcast_fusion.2
  118.5 6.0 %select_reduce_fusion.2 = f32[128,512]{1,0:T(8,128)S(1)} fusion(f32[128,128]{1,0:T(8,128)S(1)} %get-tuple-element.420, s32[128,128]{1,0:T(8,128)S(1)} %get-tuple-element.421), kind=kLoop, calls=%fused_computation.clone.1 | loop fusion | flops 25100288 | bytes 393216 | tf_op jit(solution)/shard_map/while/body/eval_jaxpr/reduce_sum | solution.py:11
  124.5 12.5 %all_gather.52 = bf16[512,128]{0,1:T(8,128)(2,1)S(1)} all-gather(bf16[128,128]{0,1:T(8,128)(2,1)S(1)} %multiply_convert_fusion.8), channel_id=1, replica_groups=mesh['member'=2,'section'=4,'atoms'=4] {'atoms'}, dimensions={0}, use_global_device_ids=true | all-gather | bytes 163840 | tf_op jit(solution)/shard_map/while/body/eval_jaxpr/all_gather | solution.py:30
  140.5 12.4 %all_gather.53 = bf16[512,128]{0,1:T(8,128)(2,1)S(1)} all-gather(bf16[128,128]{0,1:T(8,128)(2,1)S(1)} %multiply_convert_fusion.9), channel_id=1, replica_groups=mesh['member'=2,'section'=4,'atoms'=4] {'atoms'}, dimensions={0}, use_global_device_ids=true | all-gather | bytes 163840 | tf_op jit(solution)/shard_map/while/body/eval_jaxpr/all_gather | solution.py:30
  155.8 12.3 %all_gather.54 = bf16[512,128]{0,1:T(8,128)(2,1)S(1)} all-gather(bf16[128,128]{0,1:T(8,128)(2,1)S(1)} %multiply_convert_fusion.10), channel_id=1, replica_groups=mesh['member'=2,'section'=4,'atoms'=4] {'atoms'}, dimensions={0}, use_global_device_ids=true | all-gather | bytes 163840 | tf_op jit(solution)/shard_map/while/body/eval_jaxpr/all_gather | solution.py:30
  170.9 12.3 %all_gather.55 = bf16[512,128]{0,1:T(8,128)(2,1)S(1)} all-gather(bf16[128,128]{0,1:T(8,128)(2,1)S(1)} %multiply_convert_fusion.11), channel_id=1, replica_groups=mesh['member'=2,'section'=4,'atoms'=4] {'atoms'}, dimensions={0}, use_global_device_ids=true | all-gather | bytes 163840 | tf_op jit(solution)/shard_map/while/body/eval_jaxpr/all_gather | solution.py:30
  185.3 2.5 %psum.14 = f32[2,3,128]{2,0,1:T(2,128)S(1)} all-reduce(f32[2,3,128]{2,0,1:T(2,128)S(1)} %get-tuple-element.217), channel_id=1, replica_groups=mesh['member'=2,'section'=4,'atoms'=4] {'member'}, use_global_device_ids=true, to_apply=%region_8.9 | all-reduce | flops 768 | bytes 6144 | tf_op jit(solution)/shard_map/psum | solution.py:106
  188.3 2.4 %psum.15 = f32[2,128]{1,0:T(2,128)S(1)} all-reduce(f32[2,128]{1,0:T(2,128)S(1)} %get-tuple-element.285), channel_id=1, replica_groups=mesh['member'=2,'section'=4,'atoms'=4] {'member'}, use_global_device_ids=true, to_apply=%region_10.11 | all-reduce | flops 256 | bytes 2048 | tf_op jit(solution)/shard_map/psum | solution.py:108
  191.5 8.9 %pmax.7 = f32[2]{0:T(128)} all-reduce(f32[2]{0:T(128)S(1)} %get-tuple-element.283), channel_id=1, replica_groups=mesh['member'=2,'section'=4,'atoms'=4] {'atoms'}, use_global_device_ids=true, to_apply=%region_12.13 | all-reduce | flops 2 | bytes 16 | tf_op jit(solution)/shard_map/pmax | solution.py:110
  (121 shorter events, 24.3 us)
Async XLA Ops:
  0.6 47.2 %copy-start = (bf16[1,128,128]{2,1,0:T(8,128)(2,1)S(1)}, bf16[1,128,128]{2,1,0:T(8,128)(2,1)}, u32[]{:S(2)}) copy-start(bf16[1,128,128]{2,1,0:T(8,128)(2,1)} %param.15) | copy-start | bytes 98308
where the time goes:
time: 201 us; the launch traced here: 200 us
  blocking collectives  159 us (79%)
  matrix products  20.5 us (10%)
  other arithmetic  16.4 us (8%)
  local copies, waits for them, and re-layouts  3.21 us (2%)
    all_gather x8, blocking collectives, block_dev(): lax.all_gather(normed, 'atoms', axis=0, tiled=True)  98.7 us
    all_gather x1, blocking collectives, shards(): pos_all = lax.all_gather(positions, 'atoms', axis=2, tiled=True)  12.2 us
    reduce_sum x2, other arithmetic, geometry(): counts = jnp.sum(hit * mask.astype(jnp.float32)[:, :, None], 1)  11.9 us
    all_gather x1, blocking collectives, shards(): lax.all_gather(norm_gain, 'section', axis=1, tiled=True)  9.53 us
    all_gather x1, blocking collectives, shards(): lax.all_gather(proj_weight, 'section', axis=1, tiled=True)  9.27 us
    pmax x1, blocking collectives, shards(): max_dev = lax.pmax(jnp.max(atom_dev, -1), 'atoms')  8.87 us
    all_gather x1, blocking collectives, shards(): lax.all_gather(force_coef, 'section', axis=1, tiled=True)  7.81 us
    all_gather x1, blocking collectives, shards(): lax.all_gather(out_weight, 'section', axis=1, tiled=True)  7.68 us

commit v1 on v0

--- a/solution.py
+++ b/solution.py
@@ -27,7 +27,9 @@
         jnp.bfloat16
     )
     keyval = jnp.dot(
-        lax.all_gather(normed, "atoms", axis=0, tiled=True),
+        jnp.concatenate(
+            lax.all_to_all(jnp.stack([normed] * lax.axis_size("atoms")), "atoms", 0, 0), axis=0
+        ),
         proj[:, width:],
         preferred_element_type=jnp.float32,
     ).astype(jnp.bfloat16)

time: 201 us -> 176 us (0.88)
  blocking collectives: 159 us -> 61.7 us
  waiting for transfers between devices: 0 us -> 35 us
  starting transfers between devices: 0 us -> 30.2 us
  local copies, waits for them, and re-layouts: 3.21 us -> 9.51 us
    all_gather x8 -> x0, blocking collectives: 98.7 us -> none  [block_dev(): lax.all_gather(normed, 'atoms', axis=0, tiled=True)]
    all_to_all x0 -> x8, waiting for transfers between devices: none -> 35 us  [block_dev(): lax.all_to_all(jnp.stack([normed] * lax.axis_size('atoms')), 'atoms', 0, 0)]
    all_to_all x0 -> x8, starting transfers between devices: none -> 30.2 us  [block_dev(): lax.all_to_all(jnp.stack([normed] * lax.axis_size('atoms')), 'atoms', 0, 0)]
    another operation x0 -> x8, local copies, waits for them, and re-layouts: none -> 5.33 us  [block_dev(): jnp.stack([normed] * lax.axis_size('atoms'))]
  transfers between devices with their start and end apart: 0 -> 8, of which waited for: 0 -> 6; matrix products, arithmetic and copies ran while one was open for 0% -> 9% of each run, Pallas kernels for 0% -> 0%
where the time goes in v1:
time: 176 us; the launch traced here: 175 us
  blocking collectives  61.7 us (35%)
  waiting for transfers between devices  35 us (20%)
  starting transfers between devices  30.2 us (17%)
  matrix products  20.3 us (12%)
  other arithmetic  16.4 us (9%)
  local copies, waits for them, and re-layouts  9.51 us (5%)
    all_to_all x8, waiting for transfers between devices, block_dev(): lax.all_to_all(jnp.stack([normed] * lax.axis_size('atoms')), 'atoms', 0, 0)  35 us
    all_to_all x8, starting transfers between devices, block_dev(): lax.all_to_all(jnp.stack([normed] * lax.axis_size('atoms')), 'atoms', 0, 0)  30.2 us
    all_gather x1, blocking collectives, shards(): pos_all = lax.all_gather(positions, 'atoms', axis=2, tiled=True)  12.2 us
    reduce_sum x2, other arithmetic, geometry(): counts = jnp.sum(hit * mask.astype(jnp.float32)[:, :, None], 1)  11.9 us
    pmax x1, blocking collectives, shards(): max_dev = lax.pmax(jnp.max(atom_dev, -1), 'atoms')  10.3 us
    all_gather x1, blocking collectives, shards(): lax.all_gather(norm_gain, 'section', axis=1, tiled=True)  9.53 us
    all_gather x1, blocking collectives, shards(): lax.all_gather(proj_weight, 'section', axis=1, tiled=True)  9.27 us
    all_gather x1, blocking collectives, shards(): lax.all_gather(force_coef, 'section', axis=1, tiled=True)  7.81 us
  transfers between devices with their start and end apart: 8, of which 6 were waited for; matrix products, arithmetic and copies ran while one was open for 9% of the time, Pallas kernels for 0%

profile of v1, /device:TPU:0, one launch (start us, length us, event | category | flops | bytes accessed | tf_op | source)
XLA Modules:
  0.0 174.6 jit_solution(10347777580018066206)
XLA Ops:
  0.6 9.5 %all_gather.16 = bf16[1,4,128]{2,0,1:T(2,128)(2,1)S(1)} all-gather(bf16[1,1,128]{2,0,1:T(2,128)(2,1)} %bitcast.317), channel_id=1, replica_groups=mesh['member'=2,'section'=4,'atoms'=4] {'section'}, dimensions={1}, use_global_device_ids=true | all-gather | bytes 1280 | tf_op jit(solution)/shard_map/all_gather | solution.py:81
  10.2 7.8 %all_gather.18 = bf16[1,4,4]{2,0,1:T(2,128)(2,1)S(1)} all-gather(bf16[1,1,4]{2,0,1:T(2,128)(2,1)} %bitcast.318), channel_id=1, replica_groups=mesh['member'=2,'section'=4,'atoms'=4] {'section'}, dimensions={1}, use_global_device_ids=true | all-gather | bytes 40 | tf_op jit(solution)/shard_map/all_gather | solution.py:84
  18.7 12.2 %all_gather.15 = f32[8,3,512]{2,1,0:T(4,128)S(1)} all-gather(f32[8,3,128]{2,1,0:T(4,128)S(1)} %copy.47), channel_id=1, replica_groups=mesh['member'=2,'section'=4,'atoms'=4] {'atoms'}, dimensions={2}, use_global_device_ids=true | all-gather | bytes 61440 | tf_op jit(solution)/shard_map/all_gather | solution.py:79
  30.9 7.7 %all_gather.19 = bf16[1,4,128,128]{3,2,0,1:T(8,128)(2,1)S(1)} all-gather(bf16[1,1,128,128]{3,2,0,1:T(8,128)(2,1)} %bitcast.316), channel_id=1, replica_groups=mesh['member'=2,'section'=4,'atoms'=4] {'section'}, dimensions={1}, use_global_device_ids=true | all-gather | bytes 163840 | tf_op jit(solution)/shard_map/all_gather | solution.py:83
  38.6 9.3 %all_gather.17 = bf16[1,4,128,384]{3,2,0,1:T(8,128)(2,1)S(1)} all-gather(bf16[1,1,128,384]{3,2,0,1:T(8,128)(2,1)} %bitcast.315), channel_id=1, replica_groups=mesh['member'=2,'section'=4,'atoms'=4] {'section'}, dimensions={1}, use_global_device_ids=true | all-gather | bytes 491520 | tf_op jit(solution)/shard_map/all_gather | solution.py:82
  47.9 110.2 %while.13 = (s32[]{:T(128)}, f32[2,3,128]{2,0,1:T(2,128)S(1)}, s32[]{:T(128)}, f32[8,3,512]{2,1,0:T(4,128)S(1)}, f32[8,3,128]{2,1,0:T(4,128)S(1)}, /*index=5*/s3...) while((s32[]{:T(128)}, f32[2,3,128]{2,0,1:T(2,128)S(1)}, ...), condition=%wide.region_7.8_spmd, body=%wide.region_0.7_spmd.sunk | while | flops 322554368 | bytes 22231392 | solution.py:104
  49.8 3.4 %all-to-all-start = ((bf16[4,128,128]{2,1,0:T(8,128)(2,1)}), bf16[4,128,128]{2,1,0:T(8,128)(2,1)S(1)}, u32[]{:S(2)}, u32[]{:S(2)}) async-start(bf16[4,128,128]{2,1,0:T(8,128)(2,1)} %stack.48), calls=%async_computation | async-start | bytes 262144 | tf_op jit(solution)/shard_map/while/body/eval_jaxpr/all_to_all | solution.py:31
  54.4 6.0 %select_reduce_fusion.2 = f32[128,512]{1,0:T(8,128)S(1)} fusion(f32[128,128]{1,0:T(8,128)S(1)} %get-tuple-element.420, s32[128,128]{1,0:T(8,128)S(1)} %get-tuple-element.421), kind=kLoop, calls=%fused_computation.clone.1 | loop fusion | flops 25100288 | bytes 393216 | tf_op jit(solution)/shard_map/while/body/eval_jaxpr/reduce_sum | solution.py:11
  64.1 5.1 %all-to-all-start.1 = ((bf16[4,128,128]{2,1,0:T(8,128)(2,1)}), bf16[4,128,128]{2,1,0:T(8,128)(2,1)S(1)}, u32[]{:S(2)}, u32[]{:S(2)}) async-start(bf16[4,128,128]{2,1,0:T(8,128)(2,1)} %stack.49), calls=%async_computation.1 | async-start | bytes 262144 | tf_op jit(solution)/shard_map/while/body/eval_jaxpr/all_to_all | solution.py:31
  69.4 6.4 %all-to-all-done.1 = bf16[4,128,128]{2,1,0:T(8,128)(2,1)S(1)} async-done(((bf16[4,128,128]{2,1,0:T(8,128)(2,1)}), bf16[4,128,128]{2,1,0:T(8,128)(2,1)S(1)}, u32[]{:S(2)}, u32[]{:S(2)}) %all-to-all-start.1) | async-done | bytes 131104 | tf_op jit(solution)/shard_map/while/body/eval_jaxpr/all_to_all | solution.py:31
  79.3 3.4 %all-to-all-start.2 = ((bf16[4,128,128]{2,1,0:T(8,128)(2,1)}), bf16[4,128,128]{2,1,0:T(8,128)(2,1)S(1)}, u32[]{:S(2)}, u32[]{:S(2)}) async-start(bf16[4,128,128]{2,1,0:T(8,128)(2,1)} %stack.50), calls=%async_computation.2 | async-start | bytes 262144 | tf_op jit(solution)/shard_map/while/body/eval_jaxpr/all_to_all | solution.py:31
  82.9 5.9 %all-to-all-done.2 = bf16[4,128,128]{2,1,0:T(8,128)(2,1)S(1)} async-done(((bf16[4,128,128]{2,1,0:T(8,128)(2,1)}), bf16[4,128,128]{2,1,0:T(8,128)(2,1)S(1)}, u32[]{:S(2)}, u32[]{:S(2)}) %all-to-all-start.2) | async-done | bytes 131104 | tf_op jit(solution)/shard_map/while/body/eval_jaxpr/all_to_all | solution.py:31
  92.2 3.3 %all-to-all-start.3 = ((bf16[4,128,128]{2,1,0:T(8,128)(2,1)}), bf16[4,128,128]{2,1,0:T(8,128)(2,1)S(1)}, u32[]{:S(2)}, u32[]{:S(2)}) async-start(bf16[4,128,128]{2,1,0:T(8,128)(2,1)} %stack.51), calls=%async_computation.3 | async-start | bytes 262144 | tf_op jit(solution)/shard_map/while/body/eval_jaxpr/all_to_all | solution.py:31
  95.7 5.7 %all-to-all-done.3 = bf16[4,128,128]{2,1,0:T(8,128)(2,1)S(1)} async-done(((bf16[4,128,128]{2,1,0:T(8,128)(2,1)}), bf16[4,128,128]{2,1,0:T(8,128)(2,1)S(1)}, u32[]{:S(2)}, u32[]{:S(2)}) %all-to-all-start.3) | async-done | bytes 131104 | tf_op jit(solution)/shard_map/while/body/eval_jaxpr/all_to_all | solution.py:31
  105.4 3.3 %all-to-all-start = ((bf16[4,128,128]{2,1,0:T(8,128)(2,1)}), bf16[4,128,128]{2,1,0:T(8,128)(2,1)S(1)}, u32[]{:S(2)}, u32[]{:S(2)}) async-start(bf16[4,128,128]{2,1,0:T(8,128)(2,1)} %stack.48), calls=%async_computation | async-start | bytes 262144 | tf_op jit(solution)/shard_map/while/body/eval_jaxpr/all_to_all | solution.py:31
  110.0 6.0 %select_reduce_fusion.2 = f32[128,512]{1,0:T(8,128)S(1)} fusion(f32[128,128]{1,0:T(8,128)S(1)} %get-tuple-element.420, s32[128,128]{1,0:T(8,128)S(1)} %get-tuple-element.421), kind=kLoop, calls=%fused_computation.clone.1 | loop fusion | flops 25100288 | bytes 393216 | tf_op jit(solution)/shard_map/while/body/eval_jaxpr/reduce_sum | solution.py:11
  119.7 5.0 %all-to-all-start.1 = ((bf16[4,128,128]{2,1,0:T(8,128)(2,1)}), bf16[4,128,128]{2,1,0:T(8,128)(2,1)S(1)}, u32[]{:S(2)}, u32[]{:S(2)}) async-start(bf16[4,128,128]{2,1,0:T(8,128)(2,1)} %stack.49), calls=%async_computation.1 | async-start | bytes 262144 | tf_op jit(solution)/shard_map/while/body/eval_jaxpr/all_to_all | solution.py:31
  124.9 5.7 %all-to-all-done.1 = bf16[4,128,128]{2,1,0:T(8,128)(2,1)S(1)} async-done(((bf16[4,128,128]{2,1,0:T(8,128)(2,1)}), bf16[4,128,128]{2,1,0:T(8,128)(2,1)S(1)}, u32[]{:S(2)}, u32[]{:S(2)}) %all-to-all-start.1) | async-done | bytes 131104 | tf_op jit(solution)/shard_map/while/body/eval_jaxpr/all_to_all | solution.py:31
  134.1 3.3 %all-to-all-start.2 = ((bf16[4,128,128]{2,1,0:T(8,128)(2,1)}), bf16[4,128,128]{2,1,0:T(8,128)(2,1)S(1)}, u32[]{:S(2)}, u32[]{:S(2)}) async-start(bf16[4,128,128]{2,1,0:T(8,128)(2,1)} %stack.50), calls=%async_computation.2 | async-start | bytes 262144 | tf_op jit(solution)/shard_map/while/body/eval_jaxpr/all_to_all | solution.py:31
  137.6 5.7 %all-to-all-done.2 = bf16[4,128,128]{2,1,0:T(8,128)(2,1)S(1)} async-done(((bf16[4,128,128]{2,1,0:T(8,128)(2,1)}), bf16[4,128,128]{2,1,0:T(8,128)(2,1)S(1)}, u32[]{:S(2)}, u32[]{:S(2)}) %all-to-all-start.2) | async-done | bytes 131104 | tf_op jit(solution)/shard_map/while/body/eval_jaxpr/all_to_all | solution.py:31
  146.8 3.3 %all-to-all-start.3 = ((bf16[4,128,128]{2,1,0:T(8,128)(2,1)}), bf16[4,128,128]{2,1,0:T(8,128)(2,1)S(1)}, u32[]{:S(2)}, u32[]{:S(2)}) async-start(bf16[4,128,128]{2,1,0:T(8,128)(2,1)} %stack.51), calls=%async_computation.3 | async-start | bytes 262144 | tf_op jit(solution)/shard_map/while/body/eval_jaxpr/all_to_all | solution.py:31
  150.3 5.7 %all-to-all-done.3 = bf16[4,128,128]{2,1,0:T(8,128)(2,1)S(1)} async-done(((bf16[4,128,128]{2,1,0:T(8,128)(2,1)}), bf16[4,128,128]{2,1,0:T(8,128)(2,1)S(1)}, u32[]{:S(2)}, u32[]{:S(2)}) %all-to-all-start.3) | async-done | bytes 131104 | tf_op jit(solution)/shard_map/while/body/eval_jaxpr/all_to_all | solution.py:31
  158.1 2.5 %psum.14 = f32[2,3,128]{2,0,1:T(2,128)S(1)} all-reduce(f32[2,3,128]{2,0,1:T(2,128)S(1)} %get-tuple-element.217), channel_id=1, replica_groups=mesh['member'=2,'section'=4,'atoms'=4] {'member'}, use_global_device_ids=true, to_apply=%region_8.9 | all-reduce | flops 768 | bytes 6144 | tf_op jit(solution)/shard_map/psum | solution.py:108
  164.3 10.3 %pmax.7 = f32[2]{0:T(128)} all-reduce(f32[2]{0:T(128)S(1)} %get-tuple-element.283), channel_id=1, replica_groups=mesh['member'=2,'section'=4,'atoms'=4] {'atoms'}, use_global_device_ids=true, to_apply=%region_12.13 | all-reduce | flops 2 | bytes 16 | tf_op jit(solution)/shard_map/pmax | solution.py:112
  (145 shorter events, 36.8 us)
Async XLA Ops:
  0.6 47.2 %copy-start = (bf16[1,128,128]{2,1,0:T(8,128)(2,1)S(1)}, bf16[1,128,128]{2,1,0:T(8,128)(2,1)}, u32[]{:S(2)}) copy-start(bf16[1,128,128]{2,1,0:T(8,128)(2,1)} %param.15) | copy-start | bytes 98308
  49.8 10.9 %all-to-all-start = ((bf16[4,128,128]{2,1,0:T(8,128)(2,1)}), bf16[4,128,128]{2,1,0:T(8,128)(2,1)S(1)}, u32[]{:S(2)}, u32[]{:S(2)}) async-start(bf16[4,128,128]{2,1,0:T(8,128)(2,1)} %stack.48), calls=%async_computation | async-start | bytes 262144 | tf_op jit(solution)/shard_map/while/body/eval_jaxpr/all_to_all | solution.py:31
  64.1 11.7 %all-to-all-start.1 = ((bf16[4,128,128]{2,1,0:T(8,128)(2,1)}), bf16[4,128,128]{2,1,0:T(8,128)(2,1)S(1)}, u32[]{:S(2)}, u32[]{:S(2)}) async-start(bf16[4,128,128]{2,1,0:T(8,128)(2,1)} %stack.49), calls=%async_computation.1 | async-start | bytes 262144 | tf_op jit(solution)/shard_map/while/body/eval_jaxpr/all_to_all | solution.py:31
  79.3 9.5 %all-to-all-start.2 = ((bf16[4,128,128]{2,1,0:T(8,128)(2,1)}), bf16[4,128,128]{2,1,0:T(8,128)(2,1)S(1)}, u32[]{:S(2)}, u32[]{:S(2)}) async-start(bf16[4,128,128]{2,1,0:T(8,128)(2,1)} %stack.50), calls=%async_computation.2 | async-start | bytes 262144 | tf_op jit(solution)/shard_map/while/body/eval_jaxpr/all_to_all | solution.py:31
  92.2 9.2 %all-to-all-start.3 = ((bf16[4,128,128]{2,1,0:T(8,128)(2,1)}), bf16[4,128,128]{2,1,0:T(8,128)(2,1)S(1)}, u32[]{:S(2)}, u32[]{:S(2)}) async-start(bf16[4,128,128]{2,1,0:T(8,128)(2,1)} %stack.51), calls=%async_computation.3 | async-start | bytes 262144 | tf_op jit(solution)/shard_map/while/body/eval_jaxpr/all_to_all | solution.py:31
  105.4 10.8 %all-to-all-start = ((bf16[4,128,128]{2,1,0:T(8,128)(2,1)}), bf16[4,128,128]{2,1,0:T(8,128)(2,1)S(1)}, u32[]{:S(2)}, u32[]{:S(2)}) async-start(bf16[4,128,128]{2,1,0:T(8,128)(2,1)} %stack.48), calls=%async_computation | async-start | bytes 262144 | tf_op jit(solution)/shard_map/while/body/eval_jaxpr/all_to_all | solution.py:31
  119.7 10.9 %all-to-all-start.1 = ((bf16[4,128,128]{2,1,0:T(8,128)(2,1)}), bf16[4,128,128]{2,1,0:T(8,128)(2,1)S(1)}, u32[]{:S(2)}, u32[]{:S(2)}) async-start(bf16[4,128,128]{2,1,0:T(8,128)(2,1)} %stack.49), calls=%async_computation.1 | async-start | bytes 262144 | tf_op jit(solution)/shard_map/while/body/eval_jaxpr/all_to_all | solution.py:31
  134.1 9.2 %all-to-all-start.2 = ((bf16[4,128,128]{2,1,0:T(8,128)(2,1)}), bf16[4,128,128]{2,1,0:T(8,128)(2,1)S(1)}, u32[]{:S(2)}, u32[]{:S(2)}) async-start(bf16[4,128,128]{2,1,0:T(8,128)(2,1)} %stack.50), calls=%async_computation.2 | async-start | bytes 262144 | tf_op jit(solution)/shard_map/while/body/eval_jaxpr/all_to_all | solution.py:31
  146.8 9.2 %all-to-all-start.3 = ((bf16[4,128,128]{2,1,0:T(8,128)(2,1)}), bf16[4,128,128]{2,1,0:T(8,128)(2,1)S(1)}, u32[]{:S(2)}, u32[]{:S(2)}) async-start(bf16[4,128,128]{2,1,0:T(8,128)(2,1)} %stack.51), calls=%async_computation.3 | async-start | bytes 262144 | tf_op jit(solution)/shard_map/while/body/eval_jaxpr/all_to_all | solution.py:31
